TPU v7x, 32 devices: a whole 2x2x4 slice. The times are simulated.
32 devices in a mesh: grp: 4 (over x, core), shard: 8 (over z, y).
Axes of the slice: x: 2, y: 2, z: 4, core: 2. Of those that a mesh axis runs over, the one named last changes fastest.
Arguments:
- inputs: bfloat16 [16384, 1024], P(('grp', 'shard')), may hold values from -6 to 6
- cotangent: bfloat16 [16384, 1024], P(('grp', 'shard')), may hold values from -6 to 6
- doc_ids: int32 [16384], P(('grp', 'shard')), may hold values from 0 to 1, as said below
- master_in: float32 [1024, 7168], P('shard'), may hold values from -0.1875 to 0.1875
- master_out: float32 [5120, 1024], P('shard'), may hold values from -6 to 6
- vectors: float32 [12, 1024], P(None, 'shard'), may hold values from -2 to 2, as said below
- moment_in: float32 [1024, 7168], P('shard'), may hold values from -24 to 24
- moment_out: float32 [5120, 1024], P('shard'), may hold values from -24 to 24
- moment_vec: float32 [12, 1024], P(None, 'shard'), may hold values from -24 to 24
- square_in: float32 [1024, 7168], P('shard'), may hold values from 4 to 1000
- square_out: float32 [5120, 1024], P('shard'), may hold values from 4 to 1000
- square_vec: float32 [12, 1024], P(None, 'shard'), may hold values from 4 to 1000
Outputs:
- output: bfloat16 [16384, 1024], P(('grp', 'shard'))
- input_grad: float32 [16384, 1024], P(('grp', 'shard'))
- grad_in: float32 [1024, 7168], P('shard')
- grad_out: float32 [5120, 1024], P('shard')
- grad_vec: float32 [12, 1024], P(None, 'shard')
- update_in: float32 [1024, 7168], P('shard')
- update_out: float32 [5120, 1024], P('shard')
- update_vec: float32 [12, 1024], P(None, 'shard')
- moment_in_next: float32 [1024, 7168], P('shard')
- moment_out_next: float32 [5120, 1024], P('shard')
- moment_vec_next: float32 [12, 1024], P(None, 'shard')
- square_in_next: float32 [1024, 7168], P('shard')
- square_out_next: float32 [5120, 1024], P('shard')
- square_vec_next: float32 [12, 1024], P(None, 'shard')
Inputs may be any that keep to these rules, and one draw needn't show every extreme that they name: `doc_ids`: on each device the ids never fall along its 512 slots; each id j < 1 covers 8 to 512 slots in a row; id 1 covers the padding after them; on some device every sequence has 512 slots. `vectors`: rows 0 and 2 lie between 0.6 and 1.4.
All inputs are finite; a program needn't handle non-finite values.
Results may differ from a plain program's by a relative error of at most 0.035.
Values may be sent and summed in bfloat16 or wider, within the bound.
A program may use at most 320 MiB of HBM per device.

v0:
```python
import jax
import jax.numpy as jnp
from jax import lax
from jax.sharding import PartitionSpec as P

HEAD = 64
ROT = 16
SEQ_DEV = 1
STEP = 10
NEG = -1e30


def rotary_tables(doc_ids):
    count = doc_ids.shape[0]
    order = jnp.arange(count, dtype=jnp.int32)
    first = jnp.sum((doc_ids[None, :] < doc_ids[:, None]).astype(jnp.int32), axis=1)
    position = (order - first).astype(jnp.float32)
    half = ROT // 2
    freq = 10000.0 ** (-(jnp.arange(half, dtype=jnp.float32) * 2.0 / ROT))
    angle = position[:, None] * freq[None, :]
    angle = jnp.concatenate([angle, angle], axis=1)
    return (jnp.cos(angle), jnp.sin(angle))


def rotate(values, cosine, sine):
    half = ROT // 2
    part = values[..., :ROT]
    turned = jnp.concatenate([-part[..., half:], part[..., :half]], axis=-1)
    moved = part * cosine[:, None, :] + turned * sine[:, None, :]
    return jnp.concatenate([moved, values[..., ROT:]], axis=-1)


def rotate_back(grads, cosine, sine):
    half = ROT // 2
    part = grads[..., :ROT]
    scaled = part * sine[:, None, :]
    turned = jnp.concatenate([scaled[..., half:], -scaled[..., :half]], axis=-1)
    moved = part * cosine[:, None, :] + turned
    return jnp.concatenate([moved, grads[..., ROT:]], axis=-1)


def layer_norm_apply(residual_stream, norm_gain, norm_offset):
    feature_mean = jnp.mean(residual_stream, axis=-1, keepdims=True)
    mean_removed = residual_stream - feature_mean
    var = jnp.mean(mean_removed * mean_removed, axis=-1, keepdims=True)
    inverse_deviation = lax.rsqrt(var + 1e-05)
    normalized_input = mean_removed * inverse_deviation
    return (normalized_input * norm_gain + norm_offset, normalized_input, inverse_deviation)


def layer_norm_gradient(gradient_norm_output, normalized_input, inverse_deviation, norm_gain):
    gradient_normalized = gradient_norm_output * norm_gain
    gradient_stream = inverse_deviation * (
        gradient_normalized
        - jnp.mean(gradient_normalized, axis=-1, keepdims=True)
        - normalized_input
        * jnp.mean(gradient_normalized * normalized_input, axis=-1, keepdims=True)
    )
    return (
        gradient_stream,
        jnp.sum(gradient_norm_output * normalized_input, axis=0),
        jnp.sum(gradient_norm_output, axis=0),
    )


def unpack(packed, width):
    vec = packed.astype(jnp.float32)
    return (
        vec[0],
        vec[1],
        vec[2],
        vec[3],
        vec[4:7].reshape(3 * width),
        vec[7:11].reshape(4 * width),
        vec[11],
    )


def mask_block(doc_ids, start, stop):
    rows = jnp.arange(start, stop)[:, None]
    cols = jnp.arange(stop)[None, :]
    return (doc_ids[start:stop, None] == doc_ids[None, :stop]) & (cols <= rows)


def block_scores(query, keys, allowed, scale):
    raw = jnp.einsum("qhd,khd->hqk", query, keys, preferred_element_type=jnp.float32) * scale
    return jnp.where(allowed[None], raw, NEG)


def gelu_value(hidden):
    return 0.5 * hidden * (1.0 + lax.erf(hidden * 0.7071067811865476))


def gelu_slope(hidden):
    return (
        0.5 * (1.0 + lax.erf(hidden * 0.7071067811865476))
        + hidden * jnp.exp(-0.5 * hidden * hidden) * 0.3989422804014327
    )


def contract_rows(left, right):
    return lax.dot_general(
        left, right, (((0,), (0,)), ((), ())), preferred_element_type=jnp.float32
    )


def contract_cols(left, right):
    return lax.dot_general(
        left, right, (((1,), (1,)), ((), ())), preferred_element_type=jnp.float32
    )


def adam(master, moment, square, grad, decay):
    moment_next = 0.9 * moment + 0.1 * grad
    square_next = 0.95 * square + 0.05 * grad * grad
    ratio = moment_next / (1.0 - 0.9**STEP) / (jnp.sqrt(square_next / (1.0 - 0.95**STEP)) + 1e-08)
    return (-0.03 * (ratio + decay * master), moment_next, square_next)


def shards(
    inputs,
    cotangent,
    doc_ids,
    master_in,
    master_out,
    vectors,
    moment_in,
    moment_out,
    moment_vec,
    square_in,
    square_out,
    square_vec,
):
    slots, width = inputs.shape
    heads = width // HEAD
    block = min(512, slots)
    scale = HEAD ** (-0.5)
    live = (doc_ids < SEQ_DEV).astype(jnp.float32)[:, None]
    cosine, sine = rotary_tables(doc_ids)
    w_in, w_out, packed = (
        lax.all_gather(master_in.astype(jnp.bfloat16), "shard", axis=0, tiled=True),
        lax.all_gather(master_out.astype(jnp.bfloat16), "shard", axis=0, tiled=True),
        lax.all_gather(vectors.astype(jnp.bfloat16), "shard", axis=1, tiled=True),
    )
    (
        first_norm_gain,
        first_norm_offset,
        second_norm_gain,
        second_norm_offset,
        bias_qkv,
        bias_hidden,
        bias_out,
    ) = unpack(packed, width)
    residual_stream = inputs.astype(jnp.float32)
    branch_input_first, first_normalized, first_inverse_deviation = layer_norm_apply(
        residual_stream, first_norm_gain, first_norm_offset
    )
    branch_input_second, second_normalized, second_inverse_deviation = layer_norm_apply(
        residual_stream, second_norm_gain, second_norm_offset
    )
    branch_input_first = branch_input_first.astype(jnp.bfloat16)
    branch_input_second = branch_input_second.astype(jnp.bfloat16)
    qkv = (
        jnp.dot(branch_input_first, w_in[:, : 3 * width], preferred_element_type=jnp.float32)
        + bias_qkv
    )
    hidden = (
        jnp.dot(branch_input_second, w_in[:, 3 * width :], preferred_element_type=jnp.float32)
        + bias_hidden
    )
    query = rotate(qkv[:, :width].reshape(slots, heads, HEAD), cosine, sine).astype(jnp.bfloat16)
    keys = rotate(qkv[:, width : 2 * width].reshape(slots, heads, HEAD), cosine, sine).astype(
        jnp.bfloat16
    )
    values = qkv[:, 2 * width :].reshape(slots, heads, HEAD).astype(jnp.bfloat16)
    start = 0
    stop = start + block
    allowed = mask_block(doc_ids, start, stop)
    scores = block_scores(query, keys, allowed, scale)
    top = jnp.max(scores, axis=-1, keepdims=True)
    expo = jnp.exp(scores - top)
    total = jnp.sum(expo, axis=-1, keepdims=True)
    probs = (expo / total).astype(jnp.bfloat16)
    totals = [top + jnp.log(total)]
    attended_parts = jnp.einsum("hqk,khd->qhd", probs, values, preferred_element_type=jnp.float32)
    attended = attended_parts.reshape(slots, width).astype(jnp.bfloat16)
    active = gelu_value(hidden).astype(jnp.bfloat16)
    joined = jnp.concatenate([attended, active], axis=1)
    branch = jnp.dot(joined, w_out, preferred_element_type=jnp.float32) + bias_out
    output = ((residual_stream + branch) * live).astype(jnp.bfloat16)
    d_out = cotangent.astype(jnp.float32) * live
    d_out_low = d_out.astype(jnp.bfloat16)
    d_joined = contract_cols(d_out_low, w_out)
    grad_out_term = contract_rows(joined, d_out_low)
    d_attended = d_joined[:, :width].reshape(slots, heads, HEAD).astype(jnp.bfloat16)
    d_hidden = (d_joined[:, width:] * gelu_slope(hidden)).astype(jnp.bfloat16)
    d_query_parts = []
    d_keys = jnp.zeros((slots, heads, HEAD), jnp.float32)
    d_values = jnp.zeros((slots, heads, HEAD), jnp.float32)
    for number, start in enumerate(range(0, slots, block)):
        stop = start + block
        allowed = mask_block(doc_ids, start, stop)
        scores = block_scores(query, keys, allowed, scale)
        probs = jnp.exp(scores - totals[number])
        d_probs = jnp.einsum("qhd,khd->hqk", d_attended, values, preferred_element_type=jnp.float32)
        weighted = jnp.sum(probs * d_probs, axis=-1, keepdims=True)
        d_scores = (probs * (d_probs - weighted)).astype(jnp.bfloat16)
        d_query_parts.append(
            jnp.einsum("hqk,khd->qhd", d_scores, keys, preferred_element_type=jnp.float32) * scale
        )
        d_keys = d_keys.at[:stop].add(
            jnp.einsum("hqk,qhd->khd", d_scores, query, preferred_element_type=jnp.float32) * scale
        )
        d_values = d_values.at[:stop].add(
            jnp.einsum(
                "hqk,qhd->khd",
                probs.astype(jnp.bfloat16),
                d_attended,
                preferred_element_type=jnp.float32,
            )
        )
    d_query = rotate_back(d_query_parts[0], cosine, sine)
    d_keys = rotate_back(d_keys, cosine, sine)
    d_qkv = jnp.concatenate(
        [
            d_query.reshape(slots, width),
            d_keys.reshape(slots, width),
            d_values.reshape(slots, width),
        ],
        axis=1,
    ).astype(jnp.bfloat16)
    grad_in_term = jnp.concatenate(
        [contract_rows(branch_input_first, d_qkv), contract_rows(branch_input_second, d_hidden)],
        axis=1,
    )
    gradient_branch_first = contract_cols(d_qkv, w_in[:, : 3 * width])
    gradient_branch_second = contract_cols(d_hidden, w_in[:, 3 * width :])
    gradient_stream_first, gradient_gain_first, gradient_offset_first = layer_norm_gradient(
        gradient_branch_first, first_normalized, first_inverse_deviation, first_norm_gain
    )
    gradient_stream_second, gradient_gain_second, gradient_offset_second = layer_norm_gradient(
        gradient_branch_second, second_normalized, second_inverse_deviation, second_norm_gain
    )
    input_grad = d_out + gradient_stream_first + gradient_stream_second
    grad_vec_term = jnp.concatenate(
        [
            gradient_gain_first[None],
            gradient_offset_first[None],
            gradient_gain_second[None],
            gradient_offset_second[None],
            jnp.sum(d_qkv, axis=0, dtype=jnp.float32).reshape(3, width),
            jnp.sum(d_hidden, axis=0, dtype=jnp.float32).reshape(4, width),
            jnp.sum(d_out, axis=0)[None],
        ],
        axis=0,
    )
    part_in, part_out, part_vec = (
        lax.psum_scatter(
            grad_in_term.astype(jnp.bfloat16), "shard", scatter_dimension=0, tiled=True
        ).astype(jnp.float32),
        lax.psum_scatter(
            grad_out_term.astype(jnp.bfloat16), "shard", scatter_dimension=0, tiled=True
        ).astype(jnp.float32),
        lax.psum_scatter(
            grad_vec_term.astype(jnp.bfloat16), "shard", scatter_dimension=1, tiled=True
        ).astype(jnp.float32),
    )
    grad_in, grad_out, grad_vec = (
        lax.psum(part_in.astype(jnp.bfloat16), "grp").astype(jnp.float32),
        lax.psum(part_out.astype(jnp.bfloat16), "grp").astype(jnp.float32),
        lax.psum(part_vec.astype(jnp.bfloat16), "grp").astype(jnp.float32),
    )
    update_in, moment_in_next, square_in_next = adam(master_in, moment_in, square_in, grad_in, 0.1)
    update_out, moment_out_next, square_out_next = adam(
        master_out, moment_out, square_out, grad_out, 0.1
    )
    update_vec, moment_vec_next, square_vec_next = adam(
        vectors, moment_vec, square_vec, grad_vec, 0.0
    )
    return (
        output,
        input_grad,
        grad_in,
        grad_out,
        grad_vec,
        update_in,
        update_out,
        update_vec,
        moment_in_next,
        moment_out_next,
        moment_vec_next,
        square_in_next,
        square_out_next,
        square_vec_next,
    )


def solution(mesh):
    placed = (
        P(("grp", "shard"), None),
        P(("grp", "shard"), None),
        P(("grp", "shard")),
        P("shard", None),
        P("shard", None),
        P(None, "shard"),
        P("shard", None),
        P("shard", None),
        P(None, "shard"),
        P("shard", None),
        P("shard", None),
        P(None, "shard"),
    )
    return jax.shard_map(
        shards,
        mesh=mesh,
        in_specs=placed,
        out_specs=(
            P(("grp", "shard"), None),
            P(("grp", "shard"), None),
            P("shard", None),
            P("shard", None),
            P(None, "shard"),
            P("shard", None),
            P("shard", None),
            P(None, "shard"),
            P("shard", None),
            P("shard", None),
            P(None, "shard"),
            P("shard", None),
            P("shard", None),
            P(None, "shard"),
        ),
        check_vma=False,
    )
```

profile of v0, /device:TPU:0, one launch (start us, length us, event | category | flops | bytes accessed | tf_op | source)
XLA Modules:
  0.0 945.5 jit_solution(10048721570027155907)
XLA Ops:
  12.3 28.7 %all_gather.9 = bf16[12,1024]{1,0:T(8,128)(2,1)S(1)} all-gather(bf16[12,128]{1,0:T(8,128)(2,1)S(1)} %convert_element_type.105), channel_id=1, replica_groups=mesh['grp'=4,'shard'=8] {'shard'}, dimensions={1}, use_global_device_ids=true | all-gather | bytes 27648 | tf_op jit(solution)/shard_map/all_gather | solution.py:143
  45.5 170.2 %all-gather.3.cloned.1.call-done = bf16[1024,7168]{1,0:T(8,128)(2,1)} async-done(((bf16[128,7168]{1,0:T(8,128)(2,1)}), bf16[1024,7168]{1,0:T(8,128)(2,1)}) %all-gather.3.cloned.1.call-update) | async-done | bytes 14680080 | tf_op jit(solution)/shard_map/all_gather | solution.py:141
  215.7 5.8 fusion.20
  225.6 4.4 fusion.87
  241.9 7.3 fusion.91
  249.3 8.4 fusion
  257.8 7.6 fusion.55
  266.0 10.3 %multiply_convert_fusion.1 = (bf16[512,4096]{1,0:T(8,128)(2,1)S(1)}, f32[512,4096]{1,0:T(8,128)}) fusion(f32[4096]{0:T(1024)S(1)} %bitcast.61, bf16[1024,7168]{1,0:T(8,128)(2,1)} %all-gather.3.cloned.1.call-done, bf16[512,1024]{1,0:T(8,128)(2,1)S(1)} %copy-done.2, f32[1024]{0:T(1024)S(1)} %bitcast.73, f32[1024]{0:T(1024)S(1)} %bitcast.68, ...), kind=kOutput, calls=%fused_computation.19 | convolution fusion | flops 4310695936 | bytes 22048768 | tf_op jit(solution)/shard_map/dot_general | solution.py:168
  278.7 8.9 convolution_convert_fusion
  287.6 79.6 %all-gather.5.cloned.1.call-done = bf16[5120,1024]{1,0:T(8,128)(2,1)} async-done(((bf16[640,1024]{1,0:T(8,128)(2,1)}), bf16[5120,1024]{1,0:T(8,128)(2,1)}) %all-gather.5.cloned.1.call-update) | async-done | bytes 10485776 | tf_op jit(solution)/shard_map/all_gather | solution.py:142
  367.2 8.4 fusion.67
  375.7 4.0 copy-done.4
  381.1 14.4 %multiply_reduce_fusion = (f32[16,512]{1,0:T(8,128)}, f32[16,512,512]{1,2,0:T(8,128)}) fusion(f32[16,512,512]{1,2,0:T(8,128)} %get-tuple-element.110, f32[16,512]{1,0:T(8,128)} %log_add_fusion, bf16[512,16,64]{0,2,1:T(8,128)(2,1)S(1)} %bitcast.40, bf16[512,16,64]{0,2,1:T(8,128)(2,1)} %bitcast.48), kind=kOutput, calls=%fused_computation.1 | convolution fusion | flops 549445632 | bytes 35717120 | tf_op jit(solution)/shard_map/qhd,khd->hqk/dot_general | solution.py:205
  398.0 10.8 %multiply_convert_fusion = bf16[16,512,512]{1,2,0:T(8,128)(2,1)} fusion(f32[16,512,512]{1,2,0:T(8,128)} %get-tuple-element.112, f32[16,512,512]{1,2,0:T(8,128)S(1)} %bitcast.39, f32[16,512]{1,0:T(8,128)} %get-tuple-element.111, f32[16,512]{1,0:T(8,128)} %log_add_fusion), kind=kLoop, calls=%fused_computation | loop fusion | flops 16777216 | bytes 42008576 | tf_op jit(solution)/shard_map/convert_element_type | solution.py:207
  408.8 6.1 multiply_bitcast_fusion
  415.1 5.1 multiply_bitcast_fusion.1
  423.3 4.6 fusion.56
  427.9 6.0 convolution_convert_fusion.2
  433.9 8.1 fusion.85
  442.1 5.3 convolution_convert_fusion.1
  447.4 10.6 %pad_maximum_fusion = bf16[1024,7168]{1,0:T(8,128)(2,1)} fusion(bf16[1024,4096]{1,0:T(8,128)(2,1)S(1)} %convolution_convert_fusion.1, bf16[1024,3072]{1,0:T(8,128)(2,1)S(1)} %convolution_convert_fusion.2), kind=kLoop, calls=%fused_computation.7 | loop fusion | flops 29360128 | bytes 29360128 | tf_op jit(solution)/shard_map/concatenate | solution.py:232
  458.2 9.0 fusion.12
  467.3 9.4 fusion.48
  477.8 4.2 fusion.53
  483.1 64.1 %reduce-scatter.8.cloned.1.call-done = bf16[640,1024]{1,0:T(8,128)(2,1)} async-done(((bf16[5120,1024]{1,0:T(8,128)(2,1)}), bf16[640,1024]{1,0:T(8,128)(2,1)}) %reduce-scatter.8.cloned.1.call-update) | async-done | bytes 1310736 | tf_op jit(solution)/shard_map/reduce_scatter | solution.py:261
  547.2 239.2 %reduce-scatter.6.cloned.1.call-done = bf16[128,7168]{1,0:T(8,128)(2,1)} async-done(((bf16[1024,7168]{1,0:T(8,128)(2,1)}), bf16[128,7168]{1,0:T(8,128)(2,1)}) %reduce-scatter.6.cloned.1.call-update) | async-done | bytes 1835024 | tf_op jit(solution)/shard_map/reduce_scatter | solution.py:258
  786.5 11.2 %fusion.52 = bf16[512,1024]{1,0:T(8,128)(2,1)} fusion(bf16[512,1024]{1,0:T(8,128)(2,1)S(1)} %copy-done.3, bf16[5120,1024]{1,0:T(8,128)(2,1)} %all-gather.5.cloned.1.call-done, bf16[512,4096]{1,0:T(8,128)(2,1)} %copy-done.49, bf16[512,1024]{1,0:T(8,128)(2,1)S(1)} %copy-done.23, f32[512]{0:T(512)S(1)} %copy-done.40, f32[1024]{0:T(1024)S(1)} %bitcast.72), kind=kOutput, calls=%fused_computation.73 | convolution fusion | flops 5381816320 | bytes 17831936 | tf_op jit(solution)/shard_map/dot_general | solution.py:189
  797.8 53.7 %reduce-scatter.10.cloned.1.call-done = bf16[128,12]{1,0:T(8,128)(2,1)} async-done(((bf16[1024,12]{1,0:T(8,128)(2,1)}), bf16[128,12]{1,0:T(8,128)(2,1)}) %reduce-scatter.10.cloned.1.call-update) | async-done | bytes 3088
  852.2 5.7 psum.23
  858.6 62.7 %all-reduce.3.cloned.1.call-done = (bf16[128,7168]{1,0:T(8,128)(2,1)}, bf16[640,1024]{1,0:T(8,128)(2,1)}) async-done(((bf16[128,7168]{1,0:T(8,128)(2,1)}, bf16[640,1024]{1,0:T(8,128)(2,1)}), (bf16[128,7168]{1,0:T(8,128)(2,1)}, bf16[640,1024]{1,0:T(8,128)(2,1)})) %all-reduce.3.cloned.1.call-update) | async-done | bytes 3145744 | tf_op jit(solution)/shard_map/psum | solution.py:269
  921.3 10.9 %add_multiply_fusion = (f32[128,7168]{1,0:T(8,128)}, f32[128,7168]{1,0:T(8,128)}, f32[128,7168]{1,0:T(8,128)}, f32[128,7168]{1,0:T(8,128)}) fusion(f32[128,7168]{1,0:T(8,128)} %param.23, f32[128,7168]{1,0:T(8,128)} %param.26, f32[128,7168]{1,0:T(8,128)} %param.29, bf16[128,7168]{1,0:T(8,128)(2,1)} %get-tuple-element.66), kind=kLoop, calls=%fused_computation.37 | loop fusion | flops 13762560 | bytes 27525120 | tf_op jit(solution)/shard_map/mul | solution.py:117
  933.7 4.7 add_multiply_fusion.1
  (176 shorter events, 40.7 us)
Async XLA Ops:
  7.2 208.5 %all-gather.3.cloned.1.call-start = ((), (), s32[]{:S(2)}) async-start(), calls=%async_computation.3 | async-start | bytes 16515072 | tf_op jit(solution)/shard_map/all_gather | solution.py:141
  10.9 30.3 %copy-start.36 = (s32[512]{0:T(512)S(1)}, s32[512]{0:T(512)}, u32[]{:S(2)}) copy-start(s32[512]{0:T(512)} %param.22) | copy-start | bytes 6148
  10.9 356.3 %all-gather.5.cloned.1.call-start = ((), (), s32[]{:S(2)}) async-start(), calls=%async_computation.4 | async-start | bytes 11796480 | tf_op jit(solution)/shard_map/all_gather | solution.py:142
  12.2 203.5 %copy-start.2 = (bf16[512,1024]{1,0:T(8,128)(2,1)S(1)}, bf16[512,1024]{1,0:T(8,128)(2,1)}, u32[]{:S(2)}) copy-start(bf16[512,1024]{1,0:T(8,128)(2,1)} %param.20) | copy-start | bytes 3145732
  12.3 535.0 %reduce-scatter.8.cloned.1.call-start = ((), (), s32[]{:S(2)}) async-start(), calls=%async_computation.6 | async-start | bytes 11796480 | tf_op jit(solution)/shard_map/reduce_scatter | solution.py:261
  41.1 224.8 %copy-start.34 = (f32[1,8,4,128]{3,1,2,0:T(8,128)}, f32[1,8,4,128]{3,1,2,0:T(8,128)S(1)}, u32[]{:S(2)}) copy-start(f32[1,8,4,128]{3,1,2,0:T(8,128)S(1)} %copy.69) | copy-start | bytes 49156
  41.5 198.9 %copy-start.26 = (f32[512,16]{0,1:T(8,128)}, f32[512,16]{0,1:T(8,128)S(1)}, u32[]{:S(2)}) copy-start(f32[512,16]{0,1:T(8,128)S(1)} %get-tuple-element.106) | copy-start | bytes 98308
  41.5 198.9 %copy-start.28 = (f32[512,16]{0,1:T(8,128)}, f32[512,16]{0,1:T(8,128)S(1)}, u32[]{:S(2)}) copy-start(f32[512,16]{0,1:T(8,128)S(1)} %get-tuple-element.105) | copy-start | bytes 98308
  44.7 322.5 %copy-start.39 = (f32[512]{0:T(512)}, f32[512]{0:T(512)S(1)}, u32[]{:S(2)}) copy-start(f32[512]{0:T(512)S(1)} %compare_convert_fusion) | copy-start | bytes 6148
  44.7 221.2 %copy-start.41 = (f32[512]{0:T(512)}, f32[512]{0:T(512)S(1)}, u32[]{:S(2)}) copy-start(f32[512]{0:T(512)S(1)} %add_rsqrt_fusion) | copy-start | bytes 6148
  45.3 176.2 %copy-start.48 = (f32[1,1024]{1,0:T(1,128)}, f32[1,1024]{1,0:T(1,128)S(1)}, u32[]{:S(2)}) copy-start(f32[1,1024]{1,0:T(1,128)S(1)} %get-tuple-element.102) | copy-start | bytes 12292
  45.3 220.6 %copy-start.46 = (f32[1,1024]{1,0:T(1,128)}, f32[1,1024]{1,0:T(1,128)S(1)}, u32[]{:S(2)}) copy-start(f32[1,1024]{1,0:T(1,128)S(1)} %get-tuple-element.104) | copy-start | bytes 12292
  266.0 12.7 %copy-start.21 = (bf16[512,1024]{1,0:T(8,128)(2,1)S(1)}, bf16[512,1024]{1,0:T(8,128)(2,1)}, u32[]{:S(2)}) copy-start(bf16[512,1024]{1,0:T(8,128)(2,1)} %param.21) | copy-start | bytes 3145732
  287.6 498.9 %reduce-scatter.6.cloned.1.call-start = ((), (), s32[]{:S(2)}) async-start(), calls=%async_computation.5 | async-start | bytes 16515072 | tf_op jit(solution)/shard_map/reduce_scatter | solution.py:258
  381.1 14.5 %slice-start = ((s8[16777216]{0:T(1024)(128)(4,1)}), s8[4194304]{0:T(1024)(128)(4,1)S(1)}, s32[]{:S(2)}) async-start(s8[16777216]{0:T(1024)(128)(4,1)} %bitcast.38), calls=%async_computation.9 | async-start | bytes 8388608
  381.1 14.5 %slice-start.1 = ((s8[16777216]{0:T(1024)(128)(4,1)}), s8[4194304]{0:T(1024)(128)(4,1)S(1)}, s32[]{:S(2)}) async-start(s8[16777216]{0:T(1024)(128)(4,1)} %bitcast.38), calls=%async_computation.10 | async-start | bytes 8388608
  381.1 15.7 %slice-start.2 = ((s8[16777216]{0:T(1024)(128)(4,1)}), s8[4194304]{0:T(1024)(128)(4,1)S(1)}, s32[]{:S(2)}) async-start(s8[16777216]{0:T(1024)(128)(4,1)} %bitcast.38), calls=%async_computation.11 | async-start | bytes 8388608
  381.1 16.9 %slice-start.3 = ((s8[16777216]{0:T(1024)(128)(4,1)}), s8[4194304]{0:T(1024)(128)(4,1)S(1)}, s32[]{:S(2)}) async-start(s8[16777216]{0:T(1024)(128)(4,1)} %bitcast.38), calls=%async_computation.12 | async-start | bytes 8388608
  398.0 10.8 %copy-start.14 = (bf16[512,16,48]{0,2,1:T(8,128)(2,1)S(1)}, bf16[512,16,48]{0,2,1:T(8,128)(2,1)}, u32[]{:S(2)}) copy-start(bf16[512,16,48]{0,2,1:T(8,128)(2,1)} %copy-done.13) | copy-start | bytes 2359300
  398.0 10.8 %copy-start.25 = (bf16[512,16,16]{0,2,1:T(8,128)(2,1)S(1)}, bf16[512,16,16]{0,2,1:T(8,128)(2,1)}, u32[]{:S(2)}) copy-start(bf16[512,16,16]{0,2,1:T(8,128)(2,1)} %copy-done.24) | copy-start | bytes 786436
  458.1 393.3 %reduce-scatter.10.cloned.1.call-start = ((), (), s32[]{:S(2)}) async-start(), calls=%async_computation.7 | async-start | bytes 294912
  467.2 10.5 %copy-start.40 = (f32[512]{0:T(512)S(1)}, f32[512]{0:T(512)}, u32[]{:S(2)}) copy-start(f32[512]{0:T(512)} %copy-done.39) | copy-start | bytes 6148
  482.0 304.5 %copy-start.23 = (bf16[512,1024]{1,0:T(8,128)(2,1)S(1)}, bf16[512,1024]{1,0:T(8,128)(2,1)}, u32[]{:S(2)}) copy-start(bf16[512,1024]{1,0:T(8,128)(2,1)} %copy-done.22) | copy-start | bytes 3145732
  482.0 304.5 %copy-start.45 = (f32[1,1024]{1,0:T(1,128)S(1)}, f32[1,1024]{1,0:T(1,128)}, u32[]{:S(2)}) copy-start(f32[1,1024]{1,0:T(1,128)} %get-tuple-element.100) | copy-start | bytes 12292
  483.1 438.2 %all-reduce.3.cloned.1.call-start = ((), (), s32[]{:S(2)}) async-start(), calls=%async_computation.8 | async-start | bytes 6291456 | tf_op jit(solution)/shard_map/psum | solution.py:269
  786.5 71.4 %copy-start.38 = (f32[12,128]{1,0:T(8,128)S(1)}, f32[12,128]{1,0:T(8,128)}, u32[]{:S(2)}) copy-start(f32[12,128]{1,0:T(8,128)} %param.25) | copy-start | bytes 18436
  786.5 71.4 %copy-start.43 = (f32[12,128]{1,0:T(8,128)S(1)}, f32[12,128]{1,0:T(8,128)}, u32[]{:S(2)}) copy-start(f32[12,128]{1,0:T(8,128)} %param.28) | copy-start | bytes 18436
  786.5 71.4 %copy-start.44 = (f32[12,128]{1,0:T(8,128)S(1)}, f32[12,128]{1,0:T(8,128)}, u32[]{:S(2)}) copy-start(f32[12,128]{1,0:T(8,128)} %param.31) | copy-start | bytes 18436
  921.3 10.9 %copy-start.1 = (f32[640,1024]{1,0:T(8,128)S(1)}, f32[640,1024]{1,0:T(8,128)}, u32[]{:S(2)}) copy-start(f32[640,1024]{1,0:T(8,128)} %param.24) | copy-start | bytes 7864324
  921.3 10.9 %copy-start.15 = (f32[640,1024]{1,0:T(8,128)S(1)}, f32[640,1024]{1,0:T(8,128)}, u32[]{:S(2)}) copy-start(f32[640,1024]{1,0:T(8,128)} %param.27) | copy-start | bytes 7864324
  921.3 12.1 %copy-start.16 = (f32[640,1024]{1,0:T(8,128)S(1)}, f32[640,1024]{1,0:T(8,128)}, u32[]{:S(2)}) copy-start(f32[640,1024]{1,0:T(8,128)} %param.30) | copy-start | bytes 7864324
  921.3 12.4 %copy-start.18 = (bf16[640,1024]{1,0:T(8,128)(2,1)S(1)}, bf16[640,1024]{1,0:T(8,128)(2,1)}, u32[]{:S(2)}) copy-start(bf16[640,1024]{1,0:T(8,128)(2,1)} %get-tuple-element.67) | copy-start | bytes 3932164
  (28 other events, 171.9 us)
Sparse Core Ops, SparseCore 0:
  11.0 204.6 all-gather.2
  218.5 148.6 all-gather.4
  370.8 176.3 reduce-scatter.7
  550.7 235.7 reduce-scatter.5
  790.2 61.1 reduce-scatter.9
  853.8 67.4 all-reduce.2
where the time goes:
time: 956 us; the launch traced here: 945 us
  waiting for transfers between devices  670 us (70%)
  matrix products  119 us (12%)
  other arithmetic  74.3 us (8%)
  blocking collectives  34.4 us (4%)
  local copies, waits for them, and re-layouts  32.3 us (3%)
  between operations  15.2 us (2%)
    reduce_scatter x1, waiting for transfers between devices, shards(): lax.psum_scatter(grad_in_term.astype(jnp.bfloat16), 'shard', scatter_dime...  239 us
    all_gather x1, waiting for transfers between devices, shards(): lax.all_gather(master_in.astype(jnp.bfloat16), 'shard', axis=0, tiled=True)  170 us
    all_gather x1, waiting for transfers between devices, shards(): lax.all_gather(master_out.astype(jnp.bfloat16), 'shard', axis=0, tiled=True)  79.6 us
    reduce_scatter x1, waiting for transfers between devices, shards(): lax.psum_scatter(grad_out_term.astype(jnp.bfloat16), 'shard', scatter_dim...  64.1 us
    psum x1, waiting for transfers between devices, shards(): lax.psum(part_in.astype(jnp.bfloat16), 'grp').astype(jnp.float32)  62.7 us
    unnamed x7, waiting for transfers between devices  53.8 us
    all_gather x1, blocking collectives, shards(): lax.all_gather(vectors.astype(jnp.bfloat16), 'shard', axis=1, tiled=True)  28.7 us
    dot_general x3, matrix products, contract_cols(): lax.dot_general(left, right, (((1,), (1,)), ((), ())), preferred_element_...  26.9 us
  transfers between devices with their start and end apart: 6, of which 6 were waited for; matrix products, arithmetic and copies ran while one was open for 20% of the time, Pallas kernels for 0%

commit v1 on v0

--- a/solution.py
+++ b/solution.py
@@ -2,12 +2,17 @@
 import jax.numpy as jnp
 from jax import lax
 from jax.sharding import PartitionSpec as P
+from jax.lax import all_gather
 
 HEAD = 64
 ROT = 16
 SEQ_DEV = 1
 STEP = 10
 NEG = -1e30
+
+
+def _check_notes(u):
+    return jnp.sum(all_gather(u, axis_name="grp"), 0)
 
 
 def rotary_tables(doc_ids):
@@ -266,7 +271,7 @@
         ).astype(jnp.float32),
     )
     grad_in, grad_out, grad_vec = (
-        lax.psum(part_in.astype(jnp.bfloat16), "grp").astype(jnp.float32),
+        _check_notes(part_in.astype(jnp.bfloat16)).astype(jnp.float32),
         lax.psum(part_out.astype(jnp.bfloat16), "grp").astype(jnp.float32),
         lax.psum(part_vec.astype(jnp.bfloat16), "grp").astype(jnp.float32),
     )

time: 956 us -> 1130 us (1.18)
  waiting for transfers between devices: 670 us -> 851 us
    reduce_scatter x1, waiting for transfers between devices: 64.1 us -> 176 us  [shards(): lax.psum_scatter(grad_out_term.astype(jnp.bfloat16), 'shard', scatter_dim...]
    all_gather x1, waiting for transfers between devices: 79.6 us -> 151 us  [shards(): lax.all_gather(master_out.astype(jnp.bfloat16), 'shard', axis=0, tiled=True)]
    all_gather x0 -> x1, waiting for transfers between devices: none -> 45.6 us  [_check_notes(): return jnp.sum(all_gather(u, axis_name='grp'), 0)]
    reduce_scatter x1, waiting for transfers between devices: 239 us -> 210 us  [shards(): lax.psum_scatter(grad_in_term.astype(jnp.bfloat16), 'shard', scatter_dime...]
    psum x1, waiting for transfers between devices: 62.7 us -> 40.6 us  [shards(): lax.psum(part_out.astype(jnp.bfloat16), 'grp').astype(jnp.float32)]
    unnamed x7 -> x8, waiting for transfers between devices: 53.8 us -> 53.8 us
  transfers between devices with their start and end apart: 6 -> 7, of which waited for: 6 -> 7; matrix products, arithmetic and copies ran while one was open for 20% -> 4% of each run, Pallas kernels for 0% -> 0%
where the time goes in v1:
time: 1130 us; the launch traced here: 1120 us
  waiting for transfers between devices  851 us (75%)
  matrix products  126 us (11%)
  other arithmetic  73.4 us (6%)
  blocking collectives  34.6 us (3%)
  local copies, waits for them, and re-layouts  24.3 us (2%)
  between operations  15.2 us (1%)
    reduce_scatter x1, waiting for transfers between devices, shards(): lax.psum_scatter(grad_in_term.astype(jnp.bfloat16), 'shard', scatter_dime...  210 us
    reduce_scatter x1, waiting for transfers between devices, shards(): lax.psum_scatter(grad_out_term.astype(jnp.bfloat16), 'shard', scatter_dim...  176 us
    all_gather x1, waiting for transfers between devices, shards(): lax.all_gather(master_in.astype(jnp.bfloat16), 'shard', axis=0, tiled=True)  173 us
    all_gather x1, waiting for transfers between devices, shards(): lax.all_gather(master_out.astype(jnp.bfloat16), 'shard', axis=0, tiled=True)  151 us
    unnamed x8, waiting for transfers between devices  53.8 us
    all_gather x1, waiting for transfers between devices, _check_notes(): return jnp.sum(all_gather(u, axis_name='grp'), 0)  45.6 us
    psum x1, waiting for transfers between devices, shards(): lax.psum(part_out.astype(jnp.bfloat16), 'grp').astype(jnp.float32)  40.6 us
    all_gather x1, blocking collectives, shards(): lax.all_gather(vectors.astype(jnp.bfloat16), 'shard', axis=1, tiled=True)  28.7 us
  transfers between devices with their start and end apart: 7, of which 7 were waited for; matrix products, arithmetic and copies ran while one was open for 4% of the time, Pallas kernels for 0%

profile of v1, /device:TPU:0, one launch (start us, length us, event | category | flops | bytes accessed | tf_op | source)
XLA Modules:
  0.0 1124.4 jit_solution(14135593474857481716)
XLA Ops:
  10.9 28.7 %all_gather.15 = bf16[12,1024]{1,0:T(8,128)(2,1)S(1)} all-gather(bf16[12,128]{1,0:T(8,128)(2,1)S(1)} %convert_element_type.107), channel_id=1, replica_groups=mesh['grp'=4,'shard'=8] {'shard'}, dimensions={1}, use_global_device_ids=true | all-gather | bytes 27648 | tf_op jit(solution)/shard_map/all_gather | solution.py:148
  42.3 173.3 %all-gather.5.cloned.1.call-done = bf16[1024,7168]{1,0:T(8,128)(2,1)} async-done(((bf16[128,7168]{1,0:T(8,128)(2,1)}), bf16[1024,7168]{1,0:T(8,128)(2,1)}) %all-gather.5.cloned.1.call-update) | async-done | bytes 14680080 | tf_op jit(solution)/shard_map/all_gather | solution.py:146
  215.6 5.8 fusion.20
  238.6 10.0 fusion.91
  248.6 8.3 fusion
  256.9 7.5 fusion.55
  265.0 10.5 multiply_convert_fusion.1
  277.6 8.8 convolution_convert_fusion
  286.5 176.5 %reduce-scatter.8.cloned.1.call-done = bf16[640,1024]{1,0:T(8,128)(2,1)} async-done(((bf16[5120,1024]{1,0:T(8,128)(2,1)}), bf16[640,1024]{1,0:T(8,128)(2,1)}) %reduce-scatter.8.cloned.1.call-update) | async-done | bytes 1310736 | tf_op jit(solution)/shard_map/reduce_scatter | solution.py:266
  463.1 40.6 %all-reduce.2.cloned.1.call-done = bf16[640,1024]{1,0:T(8,128)(2,1)} async-done(((bf16[640,1024]{1,0:T(8,128)(2,1)}), bf16[640,1024]{1,0:T(8,128)(2,1)}) %all-reduce.2.cloned.1.call-update) | async-done | bytes 1310736 | tf_op jit(solution)/shard_map/psum | solution.py:275
  503.7 8.2 add_multiply_fusion.1
  512.0 150.6 %all-gather.7.cloned.1.call-done = bf16[5120,1024]{1,0:T(8,128)(2,1)} async-done(((bf16[640,1024]{1,0:T(8,128)(2,1)}), bf16[5120,1024]{1,0:T(8,128)(2,1)}) %all-gather.7.cloned.1.call-update) | async-done | bytes 10485776 | tf_op jit(solution)/shard_map/all_gather | solution.py:147
  662.6 8.9 fusion.67
  671.5 3.8 copy-done.3
  676.1 9.6 fusion.56
  685.7 13.9 %multiply_reduce_fusion = (f32[16,512]{1,0:T(8,128)}, f32[16,512,512]{1,2,0:T(8,128)}) fusion(f32[16,512,512]{1,2,0:T(8,128)} %get-tuple-element.109, f32[16,512]{1,0:T(8,128)} %copy-done.19, bf16[512,16,64]{0,2,1:T(8,128)(2,1)S(1)} %bitcast.42, bf16[512,16,64]{0,2,1:T(8,128)(2,1)} %bitcast.56), kind=kOutput, calls=%fused_computation.1 | convolution fusion | flops 549445632 | bytes 35717120 | tf_op jit(solution)/shard_map/qhd,khd->hqk/dot_general | solution.py:210
  699.7 10.6 multiply_convert_fusion
  710.3 6.5 multiply_bitcast_fusion
  720.3 6.5 fusion.85
  726.9 5.7 convolution_convert_fusion.1
  733.9 6.9 convolution_convert_fusion.2
  740.8 10.5 pad_maximum_fusion
  751.4 8.5 fusion.12
  760.0 9.4 fusion.48
  770.5 4.4 fusion.53
  776.1 210.3 %reduce-scatter.6.cloned.1.call-done = bf16[128,7168]{1,0:T(8,128)(2,1)} async-done(((bf16[1024,7168]{1,0:T(8,128)(2,1)}), bf16[128,7168]{1,0:T(8,128)(2,1)}) %reduce-scatter.6.cloned.1.call-update) | async-done | bytes 1835024 | tf_op jit(solution)/shard_map/reduce_scatter | solution.py:263
  986.5 11.3 %fusion.52 = bf16[512,1024]{1,0:T(8,128)(2,1)} fusion(bf16[512,1024]{1,0:T(8,128)(2,1)S(1)} %copy-done.2, bf16[5120,1024]{1,0:T(8,128)(2,1)} %all-gather.7.cloned.1.call-done, bf16[512,4096]{1,0:T(8,128)(2,1)} %copy-done.40, bf16[512,1024]{1,0:T(8,128)(2,1)S(1)} %copy-done.17, f32[512]{0:T(512)S(1)} %copy-done.30, f32[1024]{0:T(1024)S(1)} %bitcast.76), kind=kOutput, calls=%fused_computation.73 | convolution fusion | flops 5381816320 | bytes 17831936 | tf_op jit(solution)/shard_map/dot_general | solution.py:194
  997.7 53.7 %reduce-scatter.10.cloned.1.call-done = bf16[128,12]{1,0:T(8,128)(2,1)} async-done(((bf16[1024,12]{1,0:T(8,128)(2,1)}), bf16[128,12]{1,0:T(8,128)(2,1)}) %reduce-scatter.10.cloned.1.call-update) | async-done | bytes 3088
  1052.2 5.9 psum.15
  1058.7 45.6 %all-gather.9.cloned.1.call-done = bf16[512,7168]{1,0:T(8,128)(2,1)} async-done(((bf16[128,7168]{1,0:T(8,128)(2,1)}), bf16[512,7168]{1,0:T(8,128)(2,1)}) %all-gather.9.cloned.1.call-update) | async-done | bytes 7340048 | tf_op jit(solution)/shard_map/all_gather | solution.py:15
  1104.3 4.6 reduce_sum.173
  1108.9 8.4 add_multiply_fusion
  (168 shorter events, 35.5 us)
Async XLA Ops:
  7.2 32.5 %copy-start.26 = (s32[512]{0:T(512)S(1)}, s32[512]{0:T(512)}, u32[]{:S(2)}) copy-start(s32[512]{0:T(512)} %param.22) | copy-start | bytes 6148
  7.2 32.9 %copy-start.1 = (bf16[512,1024]{1,0:T(8,128)(2,1)S(1)}, bf16[512,1024]{1,0:T(8,128)(2,1)}, u32[]{:S(2)}) copy-start(bf16[512,1024]{1,0:T(8,128)(2,1)} %param.20) | copy-start | bytes 3145732
  7.2 208.4 %all-gather.5.cloned.1.call-start = ((), (), s32[]{:S(2)}) async-start(), calls=%async_computation.3 | async-start | bytes 16515072 | tf_op jit(solution)/shard_map/all_gather | solution.py:146
  10.9 452.1 %reduce-scatter.8.cloned.1.call-start = ((), (), s32[]{:S(2)}) async-start(), calls=%async_computation.6 | async-start | bytes 11796480 | tf_op jit(solution)/shard_map/reduce_scatter | solution.py:266
  39.7 225.3 %copy-start.24 = (f32[1,8,4,128]{3,1,2,0:T(8,128)}, f32[1,8,4,128]{3,1,2,0:T(8,128)S(1)}, u32[]{:S(2)}) copy-start(f32[1,8,4,128]{3,1,2,0:T(8,128)S(1)} %copy.69) | copy-start | bytes 49156
  40.1 196.4 %copy-start.20 = (f32[512,16]{0,1:T(8,128)}, f32[512,16]{0,1:T(8,128)S(1)}, u32[]{:S(2)}) copy-start(f32[512,16]{0,1:T(8,128)S(1)} %get-tuple-element.105) | copy-start | bytes 98308
  40.1 196.4 %copy-start.22 = (f32[512,16]{0,1:T(8,128)}, f32[512,16]{0,1:T(8,128)S(1)}, u32[]{:S(2)}) copy-start(f32[512,16]{0,1:T(8,128)S(1)} %get-tuple-element.104) | copy-start | bytes 98308
  40.8 621.8 %copy-start.29 = (f32[512]{0:T(512)}, f32[512]{0:T(512)S(1)}, u32[]{:S(2)}) copy-start(f32[512]{0:T(512)S(1)} %compare_convert_fusion) | copy-start | bytes 6148
  40.8 224.2 %copy-start.31 = (f32[512]{0:T(512)}, f32[512]{0:T(512)S(1)}, u32[]{:S(2)}) copy-start(f32[512]{0:T(512)S(1)} %add_rsqrt_fusion) | copy-start | bytes 6148
  41.4 180.0 %copy-start.36 = (f32[1,1024]{1,0:T(1,128)}, f32[1,1024]{1,0:T(1,128)S(1)}, u32[]{:S(2)}) copy-start(f32[1,1024]{1,0:T(1,128)S(1)} %get-tuple-element.101) | copy-start | bytes 12292
  41.4 223.6 %copy-start.38 = (f32[1,1024]{1,0:T(1,128)}, f32[1,1024]{1,0:T(1,128)S(1)}, u32[]{:S(2)}) copy-start(f32[1,1024]{1,0:T(1,128)S(1)} %get-tuple-element.103) | copy-start | bytes 12292
  236.5 20.4 %copy-start.6 = (bf16[512,1024]{0,1:T(8,128)(2,1)}, bf16[512,1024]{0,1:T(8,128)(2,1)S(1)}, u32[]{:S(2)}) copy-start(bf16[512,1024]{0,1:T(8,128)(2,1)S(1)} %copy.52) | copy-start | bytes 3145732
  265.0 10.5 copy-start.16
  265.0 12.6 %copy-start.15 = (bf16[512,1024]{1,0:T(8,128)(2,1)S(1)}, bf16[512,1024]{1,0:T(8,128)(2,1)}, u32[]{:S(2)}) copy-start(bf16[512,1024]{1,0:T(8,128)(2,1)} %param.21) | copy-start | bytes 3145732
  286.4 217.2 %copy-start.11 = (f32[640,1024]{1,0:T(8,128)S(1)}, f32[640,1024]{1,0:T(8,128)}, u32[]{:S(2)}) copy-start(f32[640,1024]{1,0:T(8,128)} %param.24) | copy-start | bytes 7864324
  286.5 217.2 %all-reduce.2.cloned.1.call-start = ((), (), s32[]{:S(2)}) async-start(), calls=%async_computation.7 | async-start | bytes 2621440 | tf_op jit(solution)/shard_map/psum | solution.py:275
  463.0 199.5 %all-gather.7.cloned.1.call-start = ((), (), s32[]{:S(2)}) async-start(), calls=%async_computation.4 | async-start | bytes 11796480 | tf_op jit(solution)/shard_map/all_gather | solution.py:147
  511.9 474.5 %reduce-scatter.6.cloned.1.call-start = ((), (), s32[]{:S(2)}) async-start(), calls=%async_computation.5 | async-start | bytes 16515072 | tf_op jit(solution)/shard_map/reduce_scatter | solution.py:263
  511.9 164.1 %copy-start.19 = (f32[16,512]{1,0:T(8,128)}, f32[16,512]{1,0:T(8,128)S(1)}, u32[]{:S(2)}) copy-start(f32[16,512]{1,0:T(8,128)S(1)} %log_add_fusion) | copy-start | bytes 98308
  676.1 23.5 %slice-start = ((s8[16777216]{0:T(1024)(128)(4,1)}), s8[4194304]{0:T(1024)(128)(4,1)S(1)}, s32[]{:S(2)}) async-start(s8[16777216]{0:T(1024)(128)(4,1)} %bitcast.39), calls=%async_computation.10 | async-start | bytes 8388608
  676.1 23.5 %slice-start.1 = ((s8[16777216]{0:T(1024)(128)(4,1)}), s8[4194304]{0:T(1024)(128)(4,1)S(1)}, s32[]{:S(2)}) async-start(s8[16777216]{0:T(1024)(128)(4,1)} %bitcast.39), calls=%async_computation.11 | async-start | bytes 8388608
  685.7 13.9 %slice-start.2 = ((s8[16777216]{0:T(1024)(128)(4,1)}), s8[4194304]{0:T(1024)(128)(4,1)S(1)}, s32[]{:S(2)}) async-start(s8[16777216]{0:T(1024)(128)(4,1)} %bitcast.39), calls=%async_computation.12 | async-start | bytes 8388608
  685.7 13.9 %slice-start.3 = ((s8[16777216]{0:T(1024)(128)(4,1)}), s8[4194304]{0:T(1024)(128)(4,1)S(1)}, s32[]{:S(2)}) async-start(s8[16777216]{0:T(1024)(128)(4,1)} %bitcast.39), calls=%async_computation.13 | async-start | bytes 8388608
  699.6 17.1 %copy-start.14 = (bf16[512,16,16]{0,2,1:T(8,128)(2,1)S(1)}, bf16[512,16,16]{0,2,1:T(8,128)(2,1)}, u32[]{:S(2)}) copy-start(bf16[512,16,16]{0,2,1:T(8,128)(2,1)} %copy-done.13) | copy-start | bytes 786436
  751.4 300.0 %reduce-scatter.10.cloned.1.call-start = ((), (), s32[]{:S(2)}) async-start(), calls=%async_computation.9 | async-start | bytes 294912
  760.0 10.5 copy-start.30
  770.5 215.9 %copy-start.17 = (bf16[512,1024]{1,0:T(8,128)(2,1)S(1)}, bf16[512,1024]{1,0:T(8,128)(2,1)}, u32[]{:S(2)}) copy-start(bf16[512,1024]{1,0:T(8,128)(2,1)} %copy-done.16) | copy-start | bytes 3145732
  770.5 215.9 %copy-start.35 = (f32[1,1024]{1,0:T(1,128)S(1)}, f32[1,1024]{1,0:T(1,128)}, u32[]{:S(2)}) copy-start(f32[1,1024]{1,0:T(1,128)} %get-tuple-element.99) | copy-start | bytes 12292
  776.0 328.3 %all-gather.9.cloned.1.call-start = ((), (), s32[]{:S(2)}) async-start(), calls=%async_computation.8 | async-start | bytes 9175040 | tf_op jit(solution)/shard_map/all_gather | solution.py:15
  986.4 71.6 %copy-start.28 = (f32[12,128]{1,0:T(8,128)S(1)}, f32[12,128]{1,0:T(8,128)}, u32[]{:S(2)}) copy-start(f32[12,128]{1,0:T(8,128)} %param.25) | copy-start | bytes 18436
  986.4 71.6 %copy-start.33 = (f32[12,128]{1,0:T(8,128)S(1)}, f32[12,128]{1,0:T(8,128)}, u32[]{:S(2)}) copy-start(f32[12,128]{1,0:T(8,128)} %param.28) | copy-start | bytes 18436
  986.5 71.6 %copy-start.34 = (f32[12,128]{1,0:T(8,128)S(1)}, f32[12,128]{1,0:T(8,128)}, u32[]{:S(2)}) copy-start(f32[12,128]{1,0:T(8,128)} %param.31) | copy-start | bytes 18436
  (23 other events, 128.6 us)
Sparse Core Ops, SparseCore 0:
  11.0 204.5 all-gather.4
  286.6 176.3 reduce-scatter.7
  465.4 38.2 all-reduce.1
  512.0 150.5 all-gather.6
  751.5 234.8 reduce-scatter.5
  990.1 61.1 reduce-scatter.9
  1052.9 51.3 all-gather.8
